TPU v7x, 32 devices: a whole 2x2x4 slice. The times are simulated.
32 devices in a mesh: tm: 4 (over y, x), space: 8 (over z, core).
Axes of the slice: x: 2, y: 2, z: 4, core: 2. Of those that a mesh axis runs over, the one named last changes fastest.
Arguments:
- fields: bfloat16 [4096, 2, 16384], P('tm', None, 'space')
- calendar_day: int32 [4096], P('tm'), may hold values from 0 to 364, as said below
- events: int32 [16, 96], replicated, may hold values from 0 to 4080, as said below
- lag_offsets: int32 [16], replicated, may hold values from 0 to 15, each once
Outputs:
- composite: float32 [16, 16, 2, 16384], P('tm', None, None, 'space')
Inputs may be any that keep to these rules, and one draw needn't show every extreme that they name: `calendar_day`: days of the year of successive record days, one or two calendar days apart. `events`: each entry is a record day; a day may repeat within a type. `lag_offsets`: each of 0 to 15 once.
All inputs are finite; a program needn't handle non-finite values.
Results may differ from a plain program's by a relative error of at most 0.0012.
Values may be sent and summed in bfloat16 or wider, within the bound.
A program may use at most 64 MiB of HBM per device.

v0:
```python
import jax
import jax.numpy as jnp
from jax import lax
from jax.sharding import PartitionSpec as P

HARMONICS = 4
TWO_PI = 6.283185307179586


def regressors(calendar_day):
    phases = calendar_day.astype(jnp.float32) * (TWO_PI / 365.25)
    columns = [jnp.ones_like(phases)]
    for harmonic in range(1, HARMONICS + 1):
        columns.append(jnp.cos(harmonic * phases))
        columns.append(jnp.sin(harmonic * phases))
    return jnp.stack(columns, axis=1).astype(jnp.bfloat16)


def solve_fit(gram_matrix, projection):
    factor = jnp.linalg.cholesky(gram_matrix)
    return jax.scipy.linalg.cho_solve((factor, True), projection)


def fit_coefficients(gram_matrix, projection):
    gram_matrix, projection = lax.psum((gram_matrix, projection), "tm")
    return solve_fit(gram_matrix, projection)


def day_counts(events, lag_offsets, first_day, length):
    lag_count = lag_offsets.shape[0]
    day_numbers = first_day - (lag_count - 1) + lax.iota(jnp.int32, length + lag_count - 1)

    def type_histogram(event_row):
        matches = event_row[:, None] == day_numbers[None, :]
        return jnp.sum(matches.astype(jnp.float32), axis=0)

    histogram = lax.map(type_histogram, events).astype(jnp.bfloat16)
    shifted = jnp.stack(
        [
            lax.slice_in_dim(
                histogram, lag_count - 1 - offset, lag_count - 1 - offset + length, axis=1
            )
            for offset in range(lag_count)
        ]
    )
    lag_select = (lag_offsets[:, None] == lax.iota(jnp.int32, lag_count)[None, :]).astype(
        jnp.bfloat16
    )
    counts = jnp.einsum("ls,set->elt", lag_select, shifted, preferred_element_type=jnp.float32)
    return counts.astype(jnp.bfloat16).reshape(-1, length)


def shards(fields, calendar_day, events, lag_offsets):
    members = events.shape[1]
    lag_count = lag_offsets.shape[0]
    local_days = fields.shape[0]
    local_points = fields.shape[2]
    record = fields.reshape(local_days, 2 * local_points)
    design = regressors(calendar_day)
    gram_matrix = jnp.dot(design.T, design, preferred_element_type=jnp.float32)
    projection = jnp.dot(design.T, record, preferred_element_type=jnp.float32)
    counts = day_counts(events, lag_offsets, lax.axis_index("tm") * local_days, local_days)
    counted_design = jnp.dot(counts, design, preferred_element_type=jnp.float32)
    coefficients = fit_coefficients(gram_matrix, projection)
    raw_part = jnp.dot(counts, record, preferred_element_type=jnp.float32)
    totals = lax.psum_scatter(
        raw_part - jnp.dot(counted_design, coefficients, precision=lax.Precision.HIGHEST),
        "tm",
        scatter_dimension=0,
        tiled=True,
    )
    maps = (totals / members).reshape(-1, lag_count, 2, local_points)
    map_sums = lax.psum(jnp.sum(maps, axis=3, keepdims=True), "space")
    return maps - map_sums / (local_points * lax.axis_size("space"))


def solution(mesh):
    return jax.shard_map(
        shards,
        mesh=mesh,
        in_specs=(P("tm", None, "space"), P("tm"), P(), P()),
        out_specs=P("tm", None, None, "space"),
        check_vma=False,
    )
```

profile of v0, /device:TPU:0, one launch (start us, length us, event | category | flops | bytes accessed | tf_op | source)
XLA Modules:
  0.0 158.4 jit_solution(3301992195058840388)
XLA Ops:
  6.5 12.0 %copy.372 = bf16[128,8,2,2048]{3,1,2,0:T(8,128)(2,1)} copy(bf16[128,8,2,2048]{3,2,1,0:T(2,128)(2,1)} %bitcast.75) | data formatting | bytes 16777216
  18.6 0.1 sine_convert_fusion
  18.8 0.1 stack.112
  18.8 5.3 %fusion.14 = f32[9,4096]{1,0:T(8,128)} fusion(bf16[1024,9]{0,1:T(8,128)(2,1)S(1)} %stack.112, bf16[1024,4096]{1,0:T(8,128)(2,1)} %bitcast.73), kind=kOutput, calls=%fused_computation.55 | convolution fusion | flops 75497472 | bytes 8554496 | tf_op jit(solution)/shard_map/dot_general | solution.py:61
  24.2 0.1 fusion.13
  24.4 15.2 %while.11 = (s32[]{:T(128)}, bf16[16,1039]{1,0:T(8,128)(2,1)S(1)}, s32[16,96]{1,0:T(8,128)}, s32[]{:T(128)}, s32[]{:T(128)}, /*index=5*/s32[]{:T(128)}) while((s32[]{:T(128)}, bf16[16,1039]{1,0:T(8,128)(2,1)S(1)}, s32[16,96]{1,0:T(8,128)}, s32[]{:T(128)}, s32[]{:T(128)}, /*index=5*/s32[]{:T(128)}) %tuple.43), condition=%wide.region_2.3_spmd.clone, body=%wide.region_0.2_spmd.clone.sunk | while | flops 299234 | bytes 19943 | solution.py:37
  24.4 0.7 dynamic-slice_bitcast_fusion.2
  25.1 0.1 convert_reduce_fusion.2
  25.2 0.1 dynamic_update_slice.6
  25.3 0.7 dynamic-slice_bitcast_fusion.2
  26.0 0.1 convert_reduce_fusion.2
  26.2 0.1 dynamic_update_slice.6
  26.3 0.7 dynamic-slice_bitcast_fusion.2
  27.0 0.1 convert_reduce_fusion.2
  27.1 0.1 dynamic_update_slice.6
  27.2 0.7 dynamic-slice_bitcast_fusion.2
  27.9 0.1 convert_reduce_fusion.2
  28.2 0.7 dynamic-slice_bitcast_fusion.2
  28.9 0.1 convert_reduce_fusion.2
  29.1 0.7 dynamic-slice_bitcast_fusion.2
  29.8 0.1 convert_reduce_fusion.2
  30.1 0.7 dynamic-slice_bitcast_fusion.2
  30.8 0.1 convert_reduce_fusion.2
  31.0 0.7 dynamic-slice_bitcast_fusion.2
  31.7 0.1 convert_reduce_fusion.2
  32.0 0.7 dynamic-slice_bitcast_fusion.2
  32.7 0.1 convert_reduce_fusion.2
  32.9 0.7 dynamic-slice_bitcast_fusion.2
  33.6 0.1 convert_reduce_fusion.2
  33.9 0.7 dynamic-slice_bitcast_fusion.2
  34.6 0.1 convert_reduce_fusion.2
  34.8 0.7 dynamic-slice_bitcast_fusion.2
  35.5 0.1 convert_reduce_fusion.2
  35.8 0.7 dynamic-slice_bitcast_fusion.2
  36.5 0.1 convert_reduce_fusion.2
  36.7 0.7 dynamic-slice_bitcast_fusion.2
  37.4 0.1 convert_reduce_fusion.2
  37.7 0.7 dynamic-slice_bitcast_fusion.2
  38.4 0.1 convert_reduce_fusion.2
  38.6 0.7 dynamic-slice_bitcast_fusion.2
  39.3 0.1 convert_reduce_fusion.2
  39.5 0.2 slice_bitcast_fusion
  40.7 1.6 %stack.103 = bf16[16,16,1024]{2,0,1:T(8,128)(2,1)S(1)} concatenate(bf16[1,16,1024]{2,0,1:T(2,128)(2,1)S(1)} %copy.350, bf16[1,16,1024]{2,0,1:T(2,128)(2,1)S(1)} %copy.351, bf16[1,16,1024]{2,0,1:T(2,128)(2,1)S(1)} %copy.352, bf16[1,16,1024]{2,0,1:T(2,128)(2,1)S(1)} %copy.353, bf16[1,16,1024]{2,0,1:T(2,128)(2,1)S(1)} %copy.354, bf16[1,16,1024]{2,0,1:T(2,128)(2,1)S(1)} %copy.355, ...), dimensions={0} | concatenate | bytes 1048576 | tf_op jit(solution)/shard_map/stack | solution.py:38
  42.4 0.4 convolution_convert_fusion
  42.7 7.7 %fusion.11 = f32[256,4096]{1,0:T(8,128)} fusion(bf16[256,1024]{1,0:T(8,128)(2,1)S(1)} %bitcast.76, bf16[1024,4096]{1,0:T(8,128)(2,1)} %bitcast.74), kind=kOutput, calls=%fused_computation.52 | convolution fusion | flops 2147483648 | bytes 13107200 | tf_op jit(solution)/shard_map/dot_general | solution.py:65
  50.4 11.7 %psum.21 = f32[9,9]{0,1:T(8,128)S(1)} all-reduce(f32[9,9]{0,1:T(8,128)S(1)} %fusion.13), channel_id=1, replica_groups=mesh['tm'=4,'space'=8] {'tm'}, use_global_device_ids=true, to_apply=%region_3.4 | all-reduce | flops 81 | bytes 648 | tf_op jit(solution)/shard_map/psum | solution.py:25
  62.1 0.1 copy.367
  62.2 0.8 cholesky.16
  63.1 0.7 compare_reduce_fusion
  63.8 0.7 fusion.2
  64.5 0.7 custom-call.10
  65.2 0.2 fusion.12
  65.5 4.7 %all-reduce.2.cloned.1.call-done = f32[9,4096]{1,0:T(8,128)} async-done(((f32[9,4096]{1,0:T(8,128)}), f32[9,4096]{1,0:T(8,128)}) %all-reduce.2.cloned.1.call-update) | async-done | bytes 147472 | tf_op jit(solution)/shard_map/psum | solution.py:25
  70.1 1.4 fusion.3
  71.5 0.4 fusion.5
  71.8 6.6 %convolution_subtract_fusion = f32[256,4096]{1,0:T(8,128)} fusion(f32[256,4096]{1,0:T(8,128)} %fusion.11, f32[256,9]{0,1:T(8,128)S(1)} %fusion.12, f32[9,4096]{1,0:T(8,128)S(1)} %fusion.5), kind=kOutput, calls=%fused_computation.4 | convolution fusion | flops 114294784 | bytes 8545280 | tf_op jit(solution)/shard_map/dot_general | solution.py:67
  78.5 52.8 %reduce-scatter.2.cloned.1.call-done = f32[64,4096]{1,0:T(8,128)} async-done(((f32[256,4096]{1,0:T(8,128)}), f32[64,4096]{1,0:T(8,128)}) %reduce-scatter.2.cloned.1.call-update) | async-done | bytes 1048592 | tf_op jit(solution)/shard_map/reduce_scatter | solution.py:66
  131.3 1.3 broadcast_multiply_fusion
  132.6 0.9 reshape.28
  133.5 0.4 reduce_sum.18
  133.8 0.1 copy.369
  133.9 16.2 %psum.23 = f32[4,16,2,1]{1,0,3,2:T(4,128)S(1)} all-reduce(f32[4,16,2,1]{1,0,3,2:T(4,128)S(1)} %bitcast.78), channel_id=1, replica_groups=mesh['tm'=4,'space'=8] {'space'}, use_global_device_ids=true, to_apply=%region_9.10 | all-reduce | flops 128 | bytes 1024 | tf_op jit(solution)/shard_map/psum | solution.py:73
  150.1 0.1 copy.370
  150.2 1.4 broadcast_subtract_fusion
  (82 shorter events, 2.2 us)
Async XLA Ops:
  6.5 63.6 %all-reduce.2.cloned.1.call-start = ((), (), s32[]{:S(2)}) async-start(), calls=%async_computation.1 | async-start | bytes 524288 | tf_op jit(solution)/shard_map/psum | solution.py:25
  6.5 12.0 %copy-start = (s32[1024]{0:T(1024)S(1)}, s32[1024]{0:T(1024)}, u32[]{:S(2)}) copy-start(s32[1024]{0:T(1024)} %param.7) | copy-start | bytes 12292
  18.8 23.5 %copy-start.1 = (s32[16]{0:T(128)S(1)}, s32[16]{0:T(128)}, u32[]{:S(2)}) copy-start(s32[16]{0:T(128)} %param.9) | copy-start | bytes 196
  24.2 107.1 %reduce-scatter.2.cloned.1.call-start = ((), (), s32[]{:S(2)}) async-start(), calls=%async_computation.2 | async-start | bytes 5242880 | tf_op jit(solution)/shard_map/reduce_scatter | solution.py:66
Sparse Core Ops, SparseCore 0:
  24.3 45.7 all-reduce.1
  78.6 52.6 reduce-scatter.1
where the time goes:
time: 159 us; the launch traced here: 158 us
  waiting for transfers between devices  57.5 us (36%)
  local copies, waits for them, and re-layouts  28.5 us (18%)
  blocking collectives  27.9 us (18%)
  matrix products  22 us (14%)
  between operations  13.7 us (9%)
  other arithmetic  8.3 us (5%)
    reduce_scatter x1, waiting for transfers between devices, shards(): lax.psum_scatter(raw_part - jnp.dot(counted_design, coefficients, precisi...  52.8 us
    psum x1, blocking collectives, shards(): map_sums = lax.psum(jnp.sum(maps, axis=3, keepdims=True), 'space')  16.2 us
    unnamed x5, local copies, waits for them, and re-layouts  12 us
    psum x1, blocking collectives, fit_coefficients(): gram_matrix, projection = lax.psum((gram_matrix, projection), 'tm')  11.7 us
    eq x16, local copies, waits for them, and re-layouts, type_histogram(): matches = event_row[:, None] == day_numbers[None, :]  11.2 us
    dot_general x1, matrix products, shards(): raw_part = jnp.dot(counts, record, preferred_element_type=jnp.float32)  7.7 us
    dot_general x1, matrix products, shards(): jnp.dot(counted_design, coefficients, precision=lax.Precision.HIGHEST)  6.61 us
    dot_general x1, matrix products, shards(): projection = jnp.dot(design.T, record, preferred_element_type=jnp.float32)  5.3 us
  transfers between devices with their start and end apart: 2, of which 2 were waited for; matrix products, arithmetic and copies ran while one was open for 18% of the time, Pallas kernels for 0%

commit v1 on v0

--- a/solution.py
+++ b/solution.py
@@ -70,7 +70,9 @@
         tiled=True,
     )
     maps = (totals / members).reshape(-1, lag_count, 2, local_points)
-    map_sums = lax.psum(jnp.sum(maps, axis=3, keepdims=True), "space")
+    block = jnp.sum(maps, axis=3, keepdims=True)
+    parts = lax.all_gather(block, "space")
+    map_sums = jnp.sum(parts, axis=0)
     return maps - map_sums / (local_points * lax.axis_size("space"))
 
 

time: 159 us -> 157 us (0.987)
  blocking collectives: 27.9 us -> 25.8 us
    psum x1 -> x0, blocking collectives: 16.2 us -> none  [shards(): map_sums = lax.psum(jnp.sum(maps, axis=3, keepdims=True), 'space')]
    all_gather x0 -> x1, blocking collectives: none -> 14.1 us  [shards(): parts = lax.all_gather(block, 'space')]
where the time goes in v1:
time: 157 us; the launch traced here: 156 us
  waiting for transfers between devices  57.5 us (37%)
  local copies, waits for them, and re-layouts  28.5 us (18%)
  blocking collectives  25.8 us (16%)
  matrix products  22 us (14%)
  between operations  13.7 us (9%)
  other arithmetic  8.32 us (5%)
    reduce_scatter x1, waiting for transfers between devices, shards(): lax.psum_scatter(raw_part - jnp.dot(counted_design, coefficients, precisi...  52.8 us
    all_gather x1, blocking collectives, shards(): parts = lax.all_gather(block, 'space')  14.1 us
    unnamed x5, local copies, waits for them, and re-layouts  12 us
    psum x1, blocking collectives, fit_coefficients(): gram_matrix, projection = lax.psum((gram_matrix, projection), 'tm')  11.7 us
    eq x16, local copies, waits for them, and re-layouts, type_histogram(): matches = event_row[:, None] == day_numbers[None, :]  11.2 us
    dot_general x1, matrix products, shards(): raw_part = jnp.dot(counts, record, preferred_element_type=jnp.float32)  7.7 us
    dot_general x1, matrix products, shards(): jnp.dot(counted_design, coefficients, precision=lax.Precision.HIGHEST)  6.61 us
    dot_general x1, matrix products, shards(): projection = jnp.dot(design.T, record, preferred_element_type=jnp.float32)  5.3 us
  transfers between devices with their start and end apart: 2, of which 2 were waited for; matrix products, arithmetic and copies ran while one was open for 18% of the time, Pallas kernels for 0%

profile of v1, /device:TPU:0, one launch (start us, length us, event | category | flops | bytes accessed | tf_op | source)
XLA Modules:
  0.0 156.4 jit_solution(2694736856170568575)
XLA Ops:
  6.5 12.0 %copy.396 = bf16[128,8,2,2048]{3,1,2,0:T(8,128)(2,1)} copy(bf16[128,8,2,2048]{3,2,1,0:T(2,128)(2,1)} %bitcast.73) | data formatting | bytes 16777216
  18.6 0.1 sine_convert_fusion
  18.8 0.1 stack.112
  18.8 5.3 %fusion.14 = f32[9,4096]{1,0:T(8,128)} fusion(bf16[1024,9]{0,1:T(8,128)(2,1)S(1)} %stack.112, bf16[1024,4096]{1,0:T(8,128)(2,1)} %bitcast.71), kind=kOutput, calls=%fused_computation.55 | convolution fusion | flops 75497472 | bytes 8554496 | tf_op jit(solution)/shard_map/dot_general | solution.py:61
  24.2 0.1 fusion.13
  24.4 15.2 %while.11 = (s32[]{:T(128)}, bf16[16,1039]{1,0:T(8,128)(2,1)S(1)}, s32[16,96]{1,0:T(8,128)}, s32[]{:T(128)}, s32[]{:T(128)}, /*index=5*/s32[]{:T(128)}) while((s32[]{:T(128)}, bf16[16,1039]{1,0:T(8,128)(2,1)S(1)}, s32[16,96]{1,0:T(8,128)}, s32[]{:T(128)}, s32[]{:T(128)}, /*index=5*/s32[]{:T(128)}) %tuple.43), condition=%wide.region_2.3_spmd.clone, body=%wide.region_0.2_spmd.clone.sunk | while | flops 299234 | bytes 19943 | solution.py:37
  24.4 0.7 dynamic-slice_bitcast_fusion.2
  25.1 0.1 convert_reduce_fusion.2
  25.2 0.1 dynamic_update_slice.6
  25.3 0.7 dynamic-slice_bitcast_fusion.2
  26.0 0.1 convert_reduce_fusion.2
  26.2 0.1 dynamic_update_slice.6
  26.3 0.7 dynamic-slice_bitcast_fusion.2
  27.0 0.1 convert_reduce_fusion.2
  27.1 0.1 dynamic_update_slice.6
  27.2 0.7 dynamic-slice_bitcast_fusion.2
  27.9 0.1 convert_reduce_fusion.2
  28.2 0.7 dynamic-slice_bitcast_fusion.2
  28.9 0.1 convert_reduce_fusion.2
  29.1 0.7 dynamic-slice_bitcast_fusion.2
  29.8 0.1 convert_reduce_fusion.2
  30.1 0.7 dynamic-slice_bitcast_fusion.2
  30.8 0.1 convert_reduce_fusion.2
  31.0 0.7 dynamic-slice_bitcast_fusion.2
  31.7 0.1 convert_reduce_fusion.2
  32.0 0.7 dynamic-slice_bitcast_fusion.2
  32.7 0.1 convert_reduce_fusion.2
  32.9 0.7 dynamic-slice_bitcast_fusion.2
  33.6 0.1 convert_reduce_fusion.2
  33.9 0.7 dynamic-slice_bitcast_fusion.2
  34.6 0.1 convert_reduce_fusion.2
  34.8 0.7 dynamic-slice_bitcast_fusion.2
  35.5 0.1 convert_reduce_fusion.2
  35.8 0.7 dynamic-slice_bitcast_fusion.2
  36.5 0.1 convert_reduce_fusion.2
  36.7 0.7 dynamic-slice_bitcast_fusion.2
  37.4 0.1 convert_reduce_fusion.2
  37.7 0.7 dynamic-slice_bitcast_fusion.2
  38.4 0.1 convert_reduce_fusion.2
  38.6 0.7 dynamic-slice_bitcast_fusion.2
  39.3 0.1 convert_reduce_fusion.2
  39.5 0.2 slice_bitcast_fusion
  40.7 1.6 %stack.103 = bf16[16,16,1024]{2,0,1:T(8,128)(2,1)S(1)} concatenate(bf16[1,16,1024]{2,0,1:T(2,128)(2,1)S(1)} %copy.373, bf16[1,16,1024]{2,0,1:T(2,128)(2,1)S(1)} %copy.374, bf16[1,16,1024]{2,0,1:T(2,128)(2,1)S(1)} %copy.375, bf16[1,16,1024]{2,0,1:T(2,128)(2,1)S(1)} %copy.376, bf16[1,16,1024]{2,0,1:T(2,128)(2,1)S(1)} %copy.377, bf16[1,16,1024]{2,0,1:T(2,128)(2,1)S(1)} %copy.378, ...), dimensions={0} | concatenate | bytes 1048576 | tf_op jit(solution)/shard_map/stack | solution.py:38
  42.4 0.4 convolution_convert_fusion
  42.7 7.7 %fusion.11 = f32[256,4096]{1,0:T(8,128)} fusion(bf16[256,1024]{1,0:T(8,128)(2,1)S(1)} %bitcast.74, bf16[1024,4096]{1,0:T(8,128)(2,1)} %bitcast.72), kind=kOutput, calls=%fused_computation.52 | convolution fusion | flops 2147483648 | bytes 13107200 | tf_op jit(solution)/shard_map/dot_general | solution.py:65
  50.4 11.7 %psum.14 = f32[9,9]{0,1:T(8,128)S(1)} all-reduce(f32[9,9]{0,1:T(8,128)S(1)} %fusion.13), channel_id=1, replica_groups=mesh['tm'=4,'space'=8] {'tm'}, use_global_device_ids=true, to_apply=%region_3.4 | all-reduce | flops 81 | bytes 648 | tf_op jit(solution)/shard_map/psum | solution.py:25
  62.1 0.1 copy.390
  62.2 0.8 cholesky.16
  63.1 0.7 compare_reduce_fusion
  63.8 0.7 fusion.2
  64.5 0.7 custom-call.10
  65.2 0.2 fusion.12
  65.5 4.7 %all-reduce.2.cloned.1.call-done = f32[9,4096]{1,0:T(8,128)} async-done(((f32[9,4096]{1,0:T(8,128)}), f32[9,4096]{1,0:T(8,128)}) %all-reduce.2.cloned.1.call-update) | async-done | bytes 147472 | tf_op jit(solution)/shard_map/psum | solution.py:25
  70.1 1.4 fusion.3
  71.5 0.4 fusion.5
  71.8 6.6 %convolution_subtract_fusion = f32[256,4096]{1,0:T(8,128)} fusion(f32[256,4096]{1,0:T(8,128)} %fusion.11, f32[256,9]{0,1:T(8,128)S(1)} %fusion.12, f32[9,4096]{1,0:T(8,128)S(1)} %fusion.5), kind=kOutput, calls=%fused_computation.4 | convolution fusion | flops 114294784 | bytes 8545280 | tf_op jit(solution)/shard_map/dot_general | solution.py:67
  78.5 52.8 %reduce-scatter.2.cloned.1.call-done = f32[64,4096]{1,0:T(8,128)} async-done(((f32[256,4096]{1,0:T(8,128)}), f32[64,4096]{1,0:T(8,128)}) %reduce-scatter.2.cloned.1.call-update) | async-done | bytes 1048592 | tf_op jit(solution)/shard_map/reduce_scatter | solution.py:66
  131.3 1.3 broadcast_multiply_fusion
  132.6 0.9 reshape.33
  133.5 0.4 reduce_sum.27
  133.8 0.1 copy.392
  133.9 14.1 %all-gather = f32[32,16,2]{1,2,0:T(2,128)S(1)} all-gather(f32[4,16,2]{1,2,0:T(2,128)S(1)} %copy.392), channel_id=2, replica_groups=mesh['tm'=4,'space'=8] {'space'}, dimensions={0}, use_global_device_ids=true | all-gather | bytes 4608 | tf_op jit(solution)/shard_map/all_gather | solution.py:74
  148.1 0.1 copy.394
  148.2 1.4 broadcast_subtract_fusion
  (83 shorter events, 2.2 us)
Async XLA Ops:
  6.5 63.6 %all-reduce.2.cloned.1.call-start = ((), (), s32[]{:S(2)}) async-start(), calls=%async_computation.1 | async-start | bytes 524288 | tf_op jit(solution)/shard_map/psum | solution.py:25
  6.5 12.0 %copy-start = (s32[1024]{0:T(1024)S(1)}, s32[1024]{0:T(1024)}, u32[]{:S(2)}) copy-start(s32[1024]{0:T(1024)} %param.7) | copy-start | bytes 12292
  18.8 23.5 %copy-start.1 = (s32[16]{0:T(128)S(1)}, s32[16]{0:T(128)}, u32[]{:S(2)}) copy-start(s32[16]{0:T(128)} %param.9) | copy-start | bytes 196
  24.2 107.1 %reduce-scatter.2.cloned.1.call-start = ((), (), s32[]{:S(2)}) async-start(), calls=%async_computation.2 | async-start | bytes 5242880 | tf_op jit(solution)/shard_map/reduce_scatter | solution.py:66
Sparse Core Ops, SparseCore 0:
  24.3 45.7 all-reduce.1
  78.6 52.6 reduce-scatter.1
